TPU v7x, 32 devices: a whole 2x2x4 slice. The times are simulated.
32 devices in a mesh: dp: 4 (over y, x), seq: 8 (over z, core).
Axes of the slice: x: 2, y: 2, z: 4, core: 2. Of those that a mesh axis runs over, the one named last changes fastest.
Arguments:
- queries: bfloat16 [4, 2048, 16, 128], P('dp', 'seq'), may hold values from -9 to 9
- keys: bfloat16 [4, 2048, 8, 128], P('dp', 'seq'), may hold values from -9 to 9
- values: bfloat16 [4, 2048, 8, 128], P('dp', 'seq'), may hold values from -6 to 6
- doc_lengths: int32 [4, 8], P('dp'), may hold values from 1 to 1536, 2048 in all within a row
Outputs:
- attended: bfloat16 [4, 2048, 16, 128], P('dp', 'seq')
- z_loss: float32 [], replicated
Inputs may be any that keep to these rules, and one draw needn't show every extreme that they name: `doc_lengths`: each row's 8 lengths add up to 2048, and its longest document has exactly 1536 tokens.
All inputs are finite; a program needn't handle non-finite values.
Results may differ from a plain program's by a relative error of at most 0.012.
Values may be sent and summed in bfloat16 or wider, within the bound.
A program may use at most 64 MiB of HBM per device.

v0:
```python
import functools
import math

import jax
import jax.numpy as jnp
import numpy as np
from jax import lax
from jax.experimental import pallas as pl
from jax.experimental.pallas import tpu as pltpu
from jax.sharding import PartitionSpec as P

WINDOW = 1024
rope_base = 500000.0
score_scale = 1.0 / 12.0
masked = -1e30
MESH = pl.DeviceIdType.MESH
CHUNKS = 4
UNROLL = 8


def tables(rows, reach, width):
    half = width // 2
    frequency = rope_base ** (-2.0 * np.arange(half) / width)
    at = np.arange(rows)[None, :] - rows * np.arange(reach + 1)[:, None]
    angles = at[..., None] * frequency
    cos = np.concatenate([np.cos(angles)] * 2, axis=-1)
    sin = np.concatenate([-np.sin(angles), np.sin(angles)], axis=-1)
    return np.stack([cos, sin], axis=1).astype(np.float32)


def body(
    n, n_dp, reach, lengths, q_hbm, k_hbm, v_hbm, tab_hbm, out, z_out,
    tab, q_raw, raw, stage, spread, q_rot, weights, peaks, totals, acc, low, bias, mine, parts_seq, mine2, parts_dp,
    load_sem, z_send, z_recv, d_send, d_recv, s_send, s_recv, p_send, p_recv,
):
    rows, heads, width = k_hbm.shape
    q_heads = q_hbm.shape[1]
    group = q_heads // heads
    hops = reach // 2
    piece = rows // CHUNKS
    me = lax.axis_index("seq")
    dp = lax.axis_index("dp")
    core = lax.rem(me, 2)
    chip = me // 2
    other = me + 1 - 2 * core
    above = me + 2
    has_above = above < n
    first = core == 0
    second = core == 1

    loads = [
        pltpu.make_async_copy(k_hbm, raw.at[0, 0], load_sem.at[0]),
        pltpu.make_async_copy(v_hbm, raw.at[1, 0], load_sem.at[1]),
        pltpu.make_async_copy(q_hbm, q_raw, load_sem.at[2]),
        pltpu.make_async_copy(tab_hbm, tab, load_sem.at[3]),
    ]
    for load in loads:
        load.start()

    barrier = pltpu.get_barrier_semaphore()

    def greet_seq(j, _):
        pl.semaphore_signal(barrier, inc=1, device_id={"seq": lax.rem(me + j, n)}, device_id_type=MESH)
        return 0

    def greet_dp(j, _):
        pl.semaphore_signal(barrier, inc=1, device_id={"dp": lax.rem(dp + j, n_dp)}, device_id_type=MESH)
        return 0

    lax.fori_loop(1, n, greet_seq, 0)
    lax.fori_loop(1, n_dp, greet_dp, 0)

    peaks[...] = jnp.full_like(peaks, masked)
    totals[...] = jnp.zeros_like(totals)
    row_at = me * rows + lax.broadcasted_iota(jnp.int32, (rows, width), 0)
    start = jnp.zeros((rows, width), jnp.int32)
    end = jnp.int32(0)
    for i in range(lengths.shape[1]):
        end = end + lengths[0, i]
        start = jnp.where(end <= row_at, end, start)
    low[...] = jnp.maximum(start, row_at - (WINDOW - 1)) - me * rows

    loads[0].wait()
    loads[1].wait()
    pl.semaphore_wait(barrier, (n - 1) + (n_dp - 1))

    def up(kind, hop, i):
        return pltpu.make_async_remote_copy(
            src_ref=raw.at[kind, 2 * hop, pl.ds(i * piece, piece)],
            dst_ref=raw.at[kind, 2 * hop + 2, pl.ds(i * piece, piece)],
            send_sem=z_send.at[kind, hop, i],
            recv_sem=z_recv.at[kind, hop, i],
            device_id={"seq": above},
            device_id_type=MESH,
        )

    def across(kind, hop, i):
        there = 2 * hop + 1 - 2 * core
        slot = hop - core
        return pltpu.make_async_remote_copy(
            src_ref=raw.at[kind, 2 * hop, pl.ds(i * piece, piece)],
            dst_ref=raw.at[kind, there, pl.ds(i * piece, piece)],
            send_sem=d_send.at[kind, slot, i],
            recv_sem=d_recv.at[kind, slot, i],
            device_id={"seq": other},
            device_id_type=MESH,
        )

    def each(low_i, high_i, do):
        def step(i, _):
            do(i)
            return 0

        lax.fori_loop(low_i, high_i, step, 0)

    def send_up(kind, hop, a, b):
        @pl.when(has_above)
        def _():
            each(a, b, lambda i: up(kind, hop, i).start())

    send_up(0, 0, 0, CHUNKS)
    send_up(1, 0, 0, 1)

    @pl.when(first)
    def _():
        for kind in range(2):
            each(0, CHUNKS, lambda i: across(kind, 0, i).start())

    def take(kind, hop, a, b):
        def one(i):
            up(kind, hop - 1, i).wait_recv()
            if hop < hops:
                @pl.when(has_above)
                def _():
                    up(kind, hop, i).start()

                across(kind, hop, i).start()
            else:
                @pl.when(second)
                def _():
                    across(kind, hop, i).start()

        each(a, b, one)

    def take_across(kind, slot, a, b):
        def one(i):
            pltpu.make_async_remote_copy(
                src_ref=raw.at[kind, 0, pl.ds(i * piece, piece)],
                dst_ref=raw.at[kind, 2 * slot + 1, pl.ds(i * piece, piece)],
                send_sem=d_send.at[kind, slot, i],
                recv_sem=d_recv.at[kind, slot, i],
                device_id={"seq": other},
                device_id_type=MESH,
            ).wait_recv()

        each(a, b, one)

    loads[2].wait()
    loads[3].wait()

    stage[...] = q_raw[...].astype(jnp.float32).reshape(rows * q_heads, width)
    scale = score_scale * math.log2(math.e)

    def turn_q(h, _):
        for g in range(group):
            x = stage[pl.ds(h * group + g, rows, stride=q_heads), :]
            turned = x * tab[0, 0] + pltpu.roll(x, width // 2, 1) * tab[0, 1]
            q_rot[h, g * rows : (g + 1) * rows, :] = (turned * scale).astype(jnp.bfloat16)
        return 0

    lax.fori_loop(0, heads, turn_q, 0)

    lane = lax.broadcasted_iota(jnp.int32, (rows, width), 1)

    def score(d):
        stage[0 : rows * heads, :] = raw[0, d].astype(jnp.float32).reshape(rows * heads, width)
        key_at = lax.broadcasted_iota(jnp.int32, (rows, rows), 1) - d * rows
        query_at = lax.broadcasted_iota(jnp.int32, (rows, rows), 0)
        seen = (key_at >= low[:, 0:1]) & (key_at <= query_at)
        bias[...] = jnp.where(seen, 0.0, masked)

        def head(h, _):
            x = stage[pl.ds(h, rows, stride=heads), :]
            k = (x * tab[d, 0] + pltpu.roll(x, width // 2, 1) * tab[d, 1]).astype(jnp.bfloat16)
            for g in range(group):
                part = slice(g * rows, (g + 1) * rows)
                s = lax.dot_general(
                    q_rot[h, part, :], k, (((1,), (1,)), ((), ())), preferred_element_type=jnp.float32
                )
                s = s + bias[...]
                m = jnp.max(s, axis=1, keepdims=True)
                p = jnp.exp2(s - m)
                t = jnp.sum(p, axis=1, keepdims=True)
                weights[d, h, part, :] = p.astype(jnp.bfloat16)
                peaks[h, part, :] = jnp.where(lane == d, m, peaks[h, part, :])
                totals[h, part, :] = jnp.where(lane == d, t, totals[h, part, :])
            return 0

        lax.fori_loop(0, heads, head, 0)

    def mix(blocks, a, b, fresh=False, last=False):
        count = b - a
        for j, d in enumerate(blocks):
            stage[j * count * heads : (j + 1) * count * heads, :] = (
                raw[1, d, a:b].astype(jnp.float32).reshape(count * heads, width)
            )

        def head(h):
            v = [
                stage[pl.ds(j * count * heads + h, count, stride=heads), :].astype(jnp.bfloat16)
                for j in range(len(blocks))
            ]
            w = [weights[d, h, :, a:b] for d in blocks]
            o = jnp.dot(jnp.concatenate(w, axis=1), jnp.concatenate(v, axis=0), preferred_element_type=jnp.float32)
            if not fresh:
                o = acc[h] + o
            if last:
                for g in range(group):
                    spread[pl.ds(h * group + g, rows, stride=q_heads), :] = o[g * rows : (g + 1) * rows]
            else:
                acc[h] = o

        def pair(i, _):
            for j in range(UNROLL):
                head(i * UNROLL + j)
            return 0

        lax.fori_loop(0, heads // UNROLL, pair, 0)

    score(0)

    @pl.when(second)
    def _():
        take_across(0, 0, 0, CHUNKS)
        score(1)

    @pl.when(chip >= 1)
    def _():
        take(0, 1, 0, CHUNKS)

    send_up(1, 0, 1, CHUNKS)

    @pl.when(chip >= 1)
    def _():
        score(2)
        take_across(0, core, 0, CHUNKS)
        score(1 + 2 * core)
        take(1, 1, 0, 1)

    @pl.when(chip >= 2)
    def _():
        take(0, 2, 0, CHUNKS)
        score(4)

        @pl.when(first)
        def _():
            take_across(0, 1, 0, CHUNKS)
            score(3)

    def settle(h, square):
        m = peaks[h]
        peak = jnp.max(m, axis=1, keepdims=True)
        a = jnp.exp2(m - peak)
        total = jnp.sum(a * totals[h], axis=1, keepdims=True)
        peaks[h] = a / total
        lse = peak * math.log(2.0) + jnp.log(total)
        return square + jnp.sum(lse * lse, axis=0, keepdims=True)

    square = lax.fori_loop(0, heads, settle, jnp.zeros((1, 1), jnp.float32))
    mine[...] = jnp.broadcast_to(square, mine.shape)
    parts_seq[me] = jnp.broadcast_to(square, mine.shape)

    def tell_seq(j):
        return pltpu.make_async_remote_copy(
            src_ref=mine, dst_ref=parts_seq.at[me], send_sem=s_send.at[j], recv_sem=s_recv.at[j],
            device_id={"seq": lax.rem(me + j, n)}, device_id_type=MESH,
        )

    def heard_seq(j):
        return pltpu.make_async_remote_copy(
            src_ref=mine, dst_ref=parts_seq.at[lax.rem(me + n - j, n)], send_sem=s_send.at[j], recv_sem=s_recv.at[j],
            device_id={"seq": lax.rem(me + j, n)}, device_id_type=MESH,
        )

    def tell_dp(j):
        return pltpu.make_async_remote_copy(
            src_ref=mine2, dst_ref=parts_dp.at[dp], send_sem=p_send.at[j], recv_sem=p_recv.at[j],
            device_id={"dp": lax.rem(dp + j, n_dp)}, device_id_type=MESH,
        )

    def heard_dp(j):
        return pltpu.make_async_remote_copy(
            src_ref=mine2, dst_ref=parts_dp.at[lax.rem(dp + n_dp - j, n_dp)], send_sem=p_send.at[j], recv_sem=p_recv.at[j],
            device_id={"dp": lax.rem(dp + j, n_dp)}, device_id_type=MESH,
        )

    @pl.when(chip >= 1)
    def _():
        take(1, 1, 1, 2)

    each(1, n, lambda j: tell_seq(j).start())

    def portion(h, _):
        for d in range(reach + 1):
            weights[d, h] = (weights[d, h].astype(jnp.float32) * peaks[h, :, d : d + 1]).astype(jnp.bfloat16)
        return 0

    lax.fori_loop(0, heads, portion, 0)

    @pl.when(chip >= 1)
    def _():
        take(1, 1, 2, CHUNKS)

    @pl.when(first)
    def _():
        mix((0,), 0, rows, fresh=True)

    @pl.when(second)
    def _():
        take_across(1, 0, 0, CHUNKS)
        mix((0, 1), 0, rows, fresh=True)

    @pl.when(chip >= 1)
    def _():
        take_across(1, core, 0, CHUNKS)
        mix((2, 1 + 2 * core), 0, rows)

    each(1, n, lambda j: heard_seq(j).wait_recv())
    column = jnp.sum(parts_seq[...], axis=0)
    mine2[...] = column
    parts_dp[dp] = column

    middle = rows // 2

    @pl.when(chip >= 2)
    def _():
        take(1, 2, 0, CHUNKS // 2)

        @pl.when(second)
        def _():
            mix((4,), 0, middle)

        @pl.when(first)
        def _():
            take_across(1, 1, 0, CHUNKS // 2)
            mix((4, 3), 0, middle)

    each(1, n_dp, lambda j: tell_dp(j).start())

    @pl.when(chip >= 2)
    def _():
        take(1, 2, CHUNKS // 2, CHUNKS)

        @pl.when(second)
        def _():
            mix((4,), middle, rows, last=True)

        @pl.when(first)
        def _():
            take_across(1, 1, CHUNKS // 2, CHUNKS)
            mix((4, 3), middle, rows, last=True)

    def give(h, _):
        for g in range(group):
            spread[pl.ds(h * group + g, rows, stride=q_heads), :] = acc[h, g * rows : (g + 1) * rows, :]
        return 0

    @pl.when(chip < 2)
    def _():
        lax.fori_loop(0, heads, give, 0)

    out[...] = spread[...].reshape(rows, q_heads, width).astype(jnp.bfloat16)

    each(1, n_dp, lambda j: heard_dp(j).wait_recv())
    z_out[0, 0] = jnp.sum(jnp.sum(parts_dp[...], axis=0)[0:1, 0:1]) / (n_dp * n * rows * q_heads)

    def sent_up(kind, hop):
        each(0, CHUNKS, lambda i: up(kind, hop, i).wait_send())

    def sent_across(kind, hop):
        each(0, CHUNKS, lambda i: across(kind, hop, i).wait_send())

    for kind in range(2):
        pl.when(has_above)(functools.partial(sent_up, kind, 0))
        pl.when(has_above & (chip >= 1))(functools.partial(sent_up, kind, 1))
        pl.when(first)(functools.partial(sent_across, kind, 0))
        pl.when(chip >= 1)(functools.partial(sent_across, kind, 1))
        pl.when(second & (chip >= 2))(functools.partial(sent_across, kind, 2))
    each(1, n, lambda j: tell_seq(j).wait_send())
    each(1, n_dp, lambda j: tell_dp(j).wait_send())


def shards(queries, keys, values, doc_lengths):
    _, rows, q_heads, width = queries.shape
    heads = keys.shape[2]
    group = q_heads // heads
    n = lax.axis_size("seq")
    n_dp = lax.axis_size("dp")
    reach = -(-(WINDOW - 1) // rows)
    assert n % 2 == 0 and reach == 4
    hops = reach // 2
    tab = jnp.asarray(tables(rows, reach, width))
    vmem = pl.BlockSpec(memory_space=pltpu.VMEM)
    smem = pl.BlockSpec(memory_space=pltpu.SMEM)
    anywhere = pl.BlockSpec(memory_space=pl.ANY)
    dma = pltpu.SemaphoreType.DMA
    out, z = pl.pallas_call(
        functools.partial(body, n, n_dp, reach),
        out_shape=(
            jax.ShapeDtypeStruct((rows, q_heads, width), jnp.bfloat16),
            jax.ShapeDtypeStruct((1, 1), jnp.float32),
        ),
        in_specs=[smem, anywhere, anywhere, anywhere, anywhere],
        out_specs=(vmem, smem),
        scratch_shapes=[
            pltpu.VMEM(tab.shape, jnp.float32),
            pltpu.VMEM((rows, q_heads, width), jnp.bfloat16),
            pltpu.VMEM((2, reach + 1, rows, heads, width), jnp.bfloat16),
            pltpu.VMEM((rows * q_heads, width), jnp.float32),
            pltpu.VMEM((rows * q_heads, width), jnp.float32),
            pltpu.VMEM((heads, group * rows, width), jnp.bfloat16),
            pltpu.VMEM((reach + 1, heads, group * rows, rows), jnp.bfloat16),
            pltpu.VMEM((heads, group * rows, width), jnp.float32),
            pltpu.VMEM((heads, group * rows, width), jnp.float32),
            pltpu.VMEM((heads, group * rows, width), jnp.float32),
            pltpu.VMEM((rows, width), jnp.int32),
            pltpu.VMEM((rows, rows), jnp.float32),
            pltpu.VMEM((8, width), jnp.float32),
            pltpu.VMEM((n, 8, width), jnp.float32),
            pltpu.VMEM((8, width), jnp.float32),
            pltpu.VMEM((n_dp, 8, width), jnp.float32),
            dma((4,)),
            dma((2, hops, CHUNKS)),
            dma((2, hops, CHUNKS)),
            dma((2, hops, CHUNKS)),
            dma((2, hops, CHUNKS)),
            dma((n,)),
            dma((n,)),
            dma((n_dp,)),
            dma((n_dp,)),
        ],
        compiler_params=pltpu.CompilerParams(
            collective_id=0, has_side_effects=True, vmem_limit_bytes=60 * 1024 * 1024
        ),
        name="attend",
    )(doc_lengths, queries[0], keys[0], values[0], tab)
    return out[None], z[0, 0]


def solution(mesh):
    placed = (
        P("dp", "seq", None, None),
        P("dp", "seq", None, None),
        P("dp", "seq", None, None),
        P("dp", None),
    )
    return jax.shard_map(
        shards,
        mesh=mesh,
        in_specs=placed,
        out_specs=(P("dp", "seq", None, None), P()),
        check_vma=False,
    )
```

profile of v0, /device:TPU:16, one launch (start us, length us, event | category | flops | bytes accessed | tf_op | source)
XLA Modules:
  0.0 60.1 jit_solution(2077668333401536177)
XLA Ops:
  0.6 55.4 %attend.1 = (bf16[256,16,128]{2,1,0:T(8,128)(2,1)}, f32[1,1]{1,0:T(1,128)}) custom-call(s32[1,8]{1,0:T(1,128)} %lengths.1, bf16[256,16,128]{2,1,0:T(8,128)(2,1)} %bitcast.5, bf16[256,8,128]{2,1,0:T(8,128)(2,1)} %bitcast.7, bf16[256,8,128]{2,1,0:T(8,128)(2,1)} %bitcast.8, f32[5,2,256,128]{3,2,1,0:T(8,128)} %constant.2.clone.tab_hbm), custom_call_target="tpu_custom_call" | custom-call | tf_op jit(solution)/shard_map/attend/pallas_call | solution.py:407
  56.0 2.4 %copy.9 = bf16[1,256,16,128]{3,2,1,0:T(8,128)(2,1)} copy(bf16[1,256,16,128]{3,2,1,0:T(8,128)(2,1)} %bitcast.6) | data formatting | bytes 2097152
where the time goes:
time: 60.3 us; the launch traced here: 60.1 us
  Pallas kernels  55.4 us (92%)
  local copies, waits for them, and re-layouts  2.37 us (4%)
  between operations  2.33 us (4%)
    pallas_call x1, Pallas kernels, shards(): pl.pallas_call(functools.partial(body, n, n_dp, reach), out_shape=(jax.Sh...  55.4 us
    unnamed x1, local copies, waits for them, and re-layouts  2.37 us

commit v1 on v0

v1 whole, which is shorter than its diff:
```python
import functools
import math

import jax
import jax.numpy as jnp
import numpy as np
from jax import lax
from jax.experimental import pallas as pl
from jax.experimental.pallas import tpu as pltpu
from jax.sharding import PartitionSpec as P

WINDOW = 1024
rope_base = 500000.0
score_scale = 1.0 / 12.0
masked = -1e30
MESH = pl.DeviceIdType.MESH
TILE = 64
WIDE = (2, 1)


def tables(rows, n, width):
    half = width // 2
    frequency = rope_base ** (-2.0 * np.arange(half) / width)
    at = np.concatenate([np.arange(rows), rows * np.arange(-(-n // 8) * 8)])
    angles = at[:, None] * frequency
    cos = np.concatenate([np.cos(angles)] * 2, axis=-1)
    sin = np.concatenate([-np.sin(angles), np.sin(angles)], axis=-1)
    return np.stack([cos, sin]).astype(np.float32)


def body(
    n, n_dp, reach, lengths_hbm, q_hbm, k_hbm, v_hbm, tab_hbm, out, z_hbm,
    lengths, z_out, tab, turn, q_raw, raw, stage, spread, q_rot, kv, scores, weights, tops, shares, bias,
    mine, parts_seq, mine2, parts_dp, told, news,
    load_sem, z_send, z_recv, d_send, d_recv, s_send, s_recv, p_send, p_recv, t_send, t_recv,
):
    rows, heads, width = k_hbm.shape
    q_heads = q_hbm.shape[1]
    group = q_heads // heads
    tall = group * rows
    hops = reach // 2
    me = lax.axis_index("seq")
    dp = lax.axis_index("dp")
    core = lax.rem(me, 2)
    chip = me // 2
    other = me + 1 - 2 * core
    above = me + 2
    has_above = above < n
    first = core == 0
    second = core == 1
    blocks = jnp.minimum(me, reach) + 1

    loads = [
        pltpu.make_async_copy(k_hbm, raw.at[0], load_sem.at[0]),
        pltpu.make_async_copy(tab_hbm, tab, load_sem.at[3]),
        pltpu.make_async_copy(v_hbm, raw.at[1], load_sem.at[1]),
        pltpu.make_async_copy(q_hbm, q_raw, load_sem.at[2]),
        pltpu.make_async_copy(lengths_hbm, lengths, load_sem.at[4]),
    ]
    for load in loads:
        load.start()

    barrier = pltpu.get_barrier_semaphore()

    def greet(axis, at):
        pl.semaphore_signal(barrier, inc=1, device_id={axis: at}, device_id_type=MESH)

    def each(low_i, high_i, do):
        def step(i, _):
            do(i)
            return 0

        lax.fori_loop(low_i, high_i, step, 0)

    has_below = me >= 2
    far = me >= 3
    lead = me == 0
    greet("seq", other)
    pl.when(has_above)(lambda: greet("seq", above))
    pl.when(has_below)(lambda: greet("seq", me - 2))

    @pl.when(lead)
    def _():
        each(3, n, lambda j: greet("seq", j))
        each(1, n_dp, lambda j: greet("dp", lax.rem(dp + j, n_dp)))

    greeted = 1 + has_above.astype(jnp.int32) + has_below.astype(jnp.int32) + far.astype(jnp.int32)
    greeted = greeted + lead.astype(jnp.int32) * (n_dp - 1)

    def up(kind, hop, h):
        return pltpu.make_async_remote_copy(
            src_ref=kv.at[kind, 2 * hop, pl.ds(h * WIDE[kind], WIDE[kind])],
            dst_ref=kv.at[kind, 2 * hop + 2, pl.ds(h * WIDE[kind], WIDE[kind])],
            send_sem=z_send.at[kind, hop, h],
            recv_sem=z_recv.at[kind, hop, h],
            device_id={"seq": above},
            device_id_type=MESH,
        )

    def across(kind, hop, h):
        there = 2 * hop + 1 - 2 * core
        slot = hop - core
        return pltpu.make_async_remote_copy(
            src_ref=kv.at[kind, 2 * hop, pl.ds(h * WIDE[kind], WIDE[kind])],
            dst_ref=kv.at[kind, there, pl.ds(h * WIDE[kind], WIDE[kind])],
            send_sem=d_send.at[kind, slot, h],
            recv_sem=d_recv.at[kind, slot, h],
            device_id={"seq": other},
            device_id_type=MESH,
        )

    def send_own(kind, h):
        @pl.when(has_above)
        def _():
            up(kind, 0, h).start()

    def share_own(kind, h):
        @pl.when(first)
        def _():
            across(kind, 0, h).start()

    def take(kind, hop, h):
        up(kind, hop - 1, h).wait_recv()
        if hop < hops:
            @pl.when(has_above)
            def _():
                up(kind, hop, h).start()

            across(kind, hop, h).start()
        else:
            @pl.when(second)
            def _():
                across(kind, hop, h).start()

    def take_across(kind, slot, h):
        pltpu.make_async_remote_copy(
            src_ref=kv.at[kind, 0, pl.ds(h * WIDE[kind], WIDE[kind])],
            dst_ref=kv.at[kind, 2 * slot + 1, pl.ds(h * WIDE[kind], WIDE[kind])],
            send_sem=d_send.at[kind, slot, h],
            recv_sem=d_recv.at[kind, slot, h],
            device_id={"seq": other},
            device_id_type=MESH,
        ).wait_recv()

    loads[0].wait()
    loads[1].wait()
    cos_b = tab[0, pl.ds(rows + me, 1), :]
    sin_b = tab[1, pl.ds(rows + me, 1), :]
    turn[0] = tab[0, 0:rows, :] * cos_b - tab[1, 0:rows, :] * sin_b
    turn[1] = tab[1, 0:rows, :] * cos_b + tab[0, 0:rows, :] * sin_b
    stage[0 : rows * heads, :] = raw[0].astype(jnp.float32).reshape(rows * heads, width)

    def turn_k(h):
        x = stage[pl.ds(h, rows, stride=heads), :]
        kv[0, 0, h] = (x * turn[0] + pltpu.roll(x, width // 2, 1) * turn[1]).astype(jnp.bfloat16)

    wide = WIDE[0]
    k_chunks, v_chunks = heads // WIDE[0], heads // WIDE[1]

    def turn_ks(i):
        for j in range(wide):
            turn_k(i * wide + j)

    turn_ks(0)
    pl.semaphore_wait(barrier, greeted)

    def first_k(i):
        @pl.when(i + 1 < k_chunks)
        def _():
            turn_ks(i + 1)

        send_own(0, i)
        share_own(0, i)

    each(0, k_chunks, first_k)
    loads[4].wait()

    row_at = me * rows + lax.broadcasted_iota(jnp.int32, (rows, rows), 0)
    start = jnp.zeros((rows, rows), jnp.int32)
    end = jnp.int32(0)
    for i in range(lengths.shape[1]):
        end = end + lengths[0, i]
        start = jnp.where(end <= row_at, end, start)
    low = jnp.maximum(start, row_at - (WINDOW - 1)) - me * rows
    query_at = lax.broadcasted_iota(jnp.int32, (rows, rows), 0)
    for d in range(reach + 1):
        key_at = lax.broadcasted_iota(jnp.int32, (rows, rows), 1) - d * rows
        bias[d] = jnp.where((key_at >= low) & (key_at <= query_at), 0.0, masked)

    loads[3].wait()
    stage[...] = q_raw[...].astype(jnp.float32).reshape(rows * q_heads, width)
    scale = score_scale * math.log2(math.e)

    def turn_q(h):
        for g in range(group):
            x = stage[pl.ds(h * group + g, rows, stride=q_heads), :]
            turned = x * turn[0] + pltpu.roll(x, width // 2, 1) * turn[1]
            q_rot[h, g * rows : (g + 1) * rows, :] = (turned * scale).astype(jnp.bfloat16)

    each(0, heads, turn_q)

    loads[2].wait()
    stage[0 : rows * heads, :] = raw[1].astype(jnp.float32).reshape(rows * heads, width)

    def move_v(h):
        kv[1, 0, h] = stage[pl.ds(h, rows, stride=heads), :].astype(jnp.bfloat16)

    each(0, heads, move_v)
    each(0, v_chunks, lambda i: share_own(1, i))

    def score(d, h, fresh=False):
        s = lax.dot_general(
            q_rot[h], kv[0, d, h], (((1,), (1,)), ((), ())), preferred_element_type=jnp.float32
        )
        for g in range(group):
            part = slice(g * rows, (g + 1) * rows)
            t = s[part] + bias[d]
            scores[h, d, part, :] = t
            top = functools.reduce(jnp.maximum, [t[:, i * width : (i + 1) * width] for i in range(rows // width)])
            tops[h, part, :] = top if fresh else jnp.maximum(tops[h, part, :], top)

    def scores_of(d, i):
        each(i * wide, (i + 1) * wide, lambda h: score(d, h))

    each(0, heads, lambda h: score(0, h, fresh=True))

    @pl.when(second)
    def _():
        def step(h):
            take_across(0, 0, h)
            scores_of(1, h)

        each(0, k_chunks, step)

    @pl.when(chip >= 1)
    def _():
        def step(h):
            take(0, 1, h)
            scores_of(2, h)

        each(0, k_chunks, step)

    each(0, v_chunks, lambda i: send_own(1, i))

    @pl.when(chip >= 1)
    def _():
        def step(h):
            take_across(0, core, h)
            scores_of(1 + 2 * core, h)

        each(0, k_chunks, step)

    @pl.when(chip >= 2)
    def _():
        def step(h):
            take(0, 2, h)
            scores_of(4, h)

        each(0, k_chunks, step)

        @pl.when(first)
        def _():
            def step(h):
                take_across(0, 1, h)
                scores_of(3, h)

            each(0, k_chunks, step)

    def finish(h, square, peak, total, part):
        shares[h, part, :] = jnp.broadcast_to(1.0 / total, (total.shape[0], width))
        lse = peak * math.log(2.0) + jnp.log(total)
        return square + jnp.sum(lse * lse, axis=0, keepdims=True)

    def weigh(h, square):
        for i in range(tall // TILE):
            part = slice(i * TILE, (i + 1) * TILE)
            peak = jnp.max(tops[h, part, :], axis=1, keepdims=True)
            total = jnp.zeros((TILE, width), jnp.float32)
            for d in range(reach + 1):
                p = jnp.exp2(scores[h, d, part, :] - peak)
                weights[h, d, part, :] = p.astype(jnp.bfloat16)
                for c in range(rows // width):
                    total = total + p[:, c * width : (c + 1) * width]
            square = finish(h, square, peak, jnp.sum(total, axis=1, keepdims=True), part)
        return square

    def weigh_some(h, square):
        for i in range(tall // TILE):
            part = slice(i * TILE, (i + 1) * TILE)
            peak = jnp.max(tops[h, part, :], axis=1, keepdims=True)

            def step(d, total):
                p = jnp.exp2(scores[h, d, part, :] - peak)
                weights[h, d, part, :] = p.astype(jnp.bfloat16)
                for c in range(rows // width):
                    total = total + p[:, c * width : (c + 1) * width]
                return total

            total = lax.fori_loop(0, blocks, step, jnp.zeros((TILE, width), jnp.float32))
            square = finish(h, square, peak, jnp.sum(total, axis=1, keepdims=True), part)
        return square

    def settle(square):
        mine[...] = jnp.broadcast_to(square, mine.shape)
        parts_seq[me] = jnp.broadcast_to(square, mine.shape)

    @pl.when(chip >= 2)
    def _():
        settle(lax.fori_loop(0, heads, weigh, jnp.zeros((1, 1), jnp.float32)))

    @pl.when(chip < 2)
    def _():
        settle(lax.fori_loop(0, heads, weigh_some, jnp.zeros((1, 1), jnp.float32)))

    def report(j):
        return pltpu.make_async_remote_copy(
            src_ref=mine, dst_ref=parts_seq.at[j], send_sem=s_send.at[0], recv_sem=s_recv.at[j],
            device_id={"seq": 0}, device_id_type=MESH,
        )

    def heard(j):
        return pltpu.make_async_remote_copy(
            src_ref=mine, dst_ref=parts_seq.at[j], send_sem=s_send.at[0], recv_sem=s_recv.at[j],
            device_id={"seq": j}, device_id_type=MESH,
        )

    def tell_dp(j):
        return pltpu.make_async_remote_copy(
            src_ref=mine2, dst_ref=parts_dp.at[dp], send_sem=p_send.at[j], recv_sem=p_recv.at[j],
            device_id={"dp": lax.rem(dp + j, n_dp)}, device_id_type=MESH,
        )

    def heard_dp(j):
        return pltpu.make_async_remote_copy(
            src_ref=mine2, dst_ref=parts_dp.at[lax.rem(dp + n_dp - j, n_dp)], send_sem=p_send.at[j], recv_sem=p_recv.at[j],
            device_id={"dp": lax.rem(dp + j, n_dp)}, device_id_type=MESH,
        )

    def tell(j):
        return pltpu.make_async_remote_copy(
            src_ref=told, dst_ref=news, send_sem=t_send.at[j], recv_sem=t_recv.at[0],
            device_id={"seq": j}, device_id_type=MESH,
        )

    @pl.when(me > 0)
    def _():
        report(me).start()

    @pl.when(chip >= 1)
    def _():
        each(0, v_chunks, lambda i: take(1, 1, i))

    @pl.when(second)
    def _():
        each(0, v_chunks, lambda i: take_across(1, 0, i))

    @pl.when(chip >= 1)
    def _():
        each(0, v_chunks, lambda i: take_across(1, core, i))

    def give(h, o):
        o = o * shares[h]
        for g in range(group):
            spread[pl.ds(h * group + g, rows, stride=q_heads), :] = o[g * rows : (g + 1) * rows]

    def mix(h):
        take(1, 2, h)

        @pl.when(first)
        def _():
            take_across(1, 1, h)

        w = jnp.concatenate([weights[h, d] for d in range(reach + 1)], axis=1)
        v = jnp.concatenate([kv[1, d, h] for d in range(reach + 1)], axis=0)
        give(h, jnp.dot(w, v, preferred_element_type=jnp.float32))

    @pl.when(chip >= 2)
    def _():
        each(0, heads - 1, mix)

    @pl.when(chip < 2)
    def _():
        def mix_some(h):
            def step(d, o):
                return o + jnp.dot(weights[h, d], kv[1, d, h], preferred_element_type=jnp.float32)

            give(h, lax.fori_loop(0, blocks, step, jnp.zeros((tall, width), jnp.float32)))

        each(0, heads, mix_some)

    @pl.when(lead)
    def _():
        each(1, n, lambda j: heard(j).wait_recv())
        column = jnp.sum(parts_seq[...], axis=0)
        mine2[...] = column
        parts_dp[dp] = column
        each(1, n_dp, lambda j: tell_dp(j).start())
        each(1, n_dp, lambda j: heard_dp(j).wait_recv())
        whole = jnp.sum(parts_dp[...], axis=0) / (n_dp * n * rows * q_heads)
        told[...] = whole
        news[...] = whole
        each(1, n, lambda j: tell(j).start())

    @pl.when(me > 0)
    def _():
        tell(me).wait_recv()

    z_out[0, 0] = jnp.sum(news[0:1, 0:1])
    save = pltpu.make_async_copy(z_out, z_hbm, load_sem.at[5])
    save.start()

    def sent_up(kind, hop, a, b):
        each(a, b, lambda i: up(kind, hop, i).wait_send())

    def sent_across(kind, hop, a, b):
        each(a, b, lambda i: across(kind, hop, i).wait_send())

    chunks = (k_chunks, v_chunks)
    for kind in range(2):
        pl.when(has_above)(functools.partial(sent_up, kind, 0, 0, chunks[kind]))
        pl.when(first)(functools.partial(sent_across, kind, 0, 0, chunks[kind]))
        pl.when(chip >= 1)(functools.partial(sent_across, kind, 1, 0, chunks[kind]))
    pl.when(has_above & (chip >= 1))(functools.partial(sent_up, 0, 1, 0, k_chunks))
    pl.when(second & (chip >= 2))(functools.partial(sent_across, 0, 2, 0, k_chunks))

    @pl.when(me > 0)
    def _():
        report(me).wait_send()

    @pl.when(lead)
    def _():
        each(1, n_dp, lambda j: tell_dp(j).wait_send())
        each(1, n, lambda j: tell(j).wait_send())

    @pl.when(chip >= 2)
    def _():
        mix(heads - 1)

    out[...] = spread[...].reshape(rows, q_heads, width).astype(jnp.bfloat16)
    pl.when(has_above & (chip >= 1))(functools.partial(sent_up, 1, 1, 0, v_chunks))
    pl.when(second & (chip >= 2))(functools.partial(sent_across, 1, 2, 0, v_chunks))
    save.wait()


def shards(queries, keys, values, lengths):
    _, rows, q_heads, width = queries.shape
    heads = keys.shape[2]
    group = q_heads // heads
    n = lax.axis_size("seq")
    n_dp = lax.axis_size("dp")
    reach = -(-(WINDOW - 1) // rows)
    assert n % 2 == 0 and reach == 4
    hops = reach // 2
    tab = jnp.asarray(tables(rows, n, width))
    vmem = pl.BlockSpec(memory_space=pltpu.VMEM)
    anywhere = pl.BlockSpec(memory_space=pl.ANY)
    dma = pltpu.SemaphoreType.DMA
    out, z = pl.pallas_call(
        functools.partial(body, n, n_dp, reach),
        out_shape=(
            pltpu.VMEM((rows, q_heads, width), jnp.bfloat16),
            jax.ShapeDtypeStruct((1, 1), jnp.float32),
        ),
        in_specs=[anywhere] * 5,
        out_specs=(vmem, anywhere),
        scratch_shapes=[
            pltpu.SMEM(lengths.shape, jnp.int32),
            pltpu.SMEM((1, 1), jnp.float32),
            pltpu.VMEM(tab.shape, jnp.float32),
            pltpu.VMEM((2, rows, width), jnp.float32),
            pltpu.VMEM((rows, q_heads, width), jnp.bfloat16),
            pltpu.VMEM((2, rows, heads, width), jnp.bfloat16),
            pltpu.VMEM((rows * q_heads, width), jnp.float32),
            pltpu.VMEM((rows * q_heads, width), jnp.float32),
            pltpu.VMEM((heads, group * rows, width), jnp.bfloat16),
            pltpu.VMEM((2, reach + 1, heads, rows, width), jnp.bfloat16),
            pltpu.VMEM((heads, reach + 1, group * rows, rows), jnp.float32),
            pltpu.VMEM((heads, reach + 1, group * rows, rows), jnp.bfloat16),
            pltpu.VMEM((heads, group * rows, width), jnp.float32),
            pltpu.VMEM((heads, group * rows, width), jnp.float32),
            pltpu.VMEM((reach + 1, rows, rows), jnp.float32),
            pltpu.VMEM((8, width), jnp.float32),
            pltpu.VMEM((n, 8, width), jnp.float32),
            pltpu.VMEM((8, width), jnp.float32),
            pltpu.VMEM((n_dp, 8, width), jnp.float32),
            pltpu.VMEM((8, width), jnp.float32),
            pltpu.VMEM((8, width), jnp.float32),
            dma((6,)),
            dma((2, hops, heads)),
            dma((2, hops, heads)),
            dma((2, hops, heads)),
            dma((2, hops, heads)),
            dma((n,)),
            dma((n,)),
            dma((n_dp,)),
            dma((n_dp,)),
            dma((n,)),
            dma((1,)),
        ],
        compiler_params=pltpu.CompilerParams(
            collective_id=0, has_side_effects=True, vmem_limit_bytes=56 * 1024 * 1024
        ),
        name="attend",
    )(lengths, queries[0], keys[0], values[0], tab)
    return out[None], z[0, 0]


def solution(mesh):
    placed = (
        P("dp", "seq", None, None),
        P("dp", "seq", None, None),
        P("dp", "seq", None, None),
        P("dp", None),
    )
    return jax.shard_map(
        shards,
        mesh=mesh,
        in_specs=placed,
        out_specs=(P("dp", "seq", None, None), P()),
        check_vma=False,
    )
```

time: 60.3 us -> 53.6 us (0.89)
  Pallas kernels: 55.4 us -> 50.2 us
  local copies, waits for them, and re-layouts: 2.37 us -> 0.97 us
    pallas_call x1, Pallas kernels: 55.4 us -> 50.2 us  [shards(): pl.pallas_call(functools.partial(body, n, n_dp, reach), out_shape=(pltpu....]
    unnamed x1, local copies, waits for them, and re-layouts: 2.37 us -> 0.97 us
where the time goes in v1:
time: 53.6 us; the launch traced here: 53.5 us
  Pallas kernels  50.2 us (94%)
  between operations  2.33 us (4%)
  local copies, waits for them, and re-layouts  0.97 us (2%)
    pallas_call x1, Pallas kernels, shards(): pl.pallas_call(functools.partial(body, n, n_dp, reach), out_shape=(pltpu....  50.2 us

profile of v1, /device:TPU:16, one launch (start us, length us, event | category | flops | bytes accessed | tf_op | source)
XLA Modules:
  0.0 53.5 jit_solution(15560318534275433348)
XLA Ops:
  0.6 50.2 %attend.1 = (bf16[256,16,128]{2,1,0:T(8,128)(2,1)S(1)}, f32[1,1]{1,0:T(1,128)}) custom-call(s32[1,8]{1,0:T(1,128)} %lengths_hbm.1, bf16[256,16,128]{2,1,0:T(8,128)(2,1)} %bitcast.6, bf16[256,8,128]{2,1,0:T(8,128)(2,1)} %bitcast.7, bf16[256,8,128]{2,1,0:T(8,128)(2,1)} %bitcast.8, f32[2,264,128]{2,1,0:T(8,128)} %constant.2.clone.tab_hbm), custom_call_target="tpu_custom_call" | custom-call | tf_op jit(solution)/shard_map/attend/pallas_call | solution.py:458
  50.8 1.0 %copy.9 = bf16[1,256,16,128]{3,2,1,0:T(8,128)(2,1)} copy(bf16[1,256,16,128]{3,2,1,0:T(8,128)(2,1)S(1)} %bitcast.5) | data formatting | bytes 2097152

commit v2 on v1

v2 whole, which is shorter than its diff:
```python
import functools
import math

import jax
import jax.numpy as jnp
import numpy as np
from jax import lax
from jax.experimental import pallas as pl
from jax.experimental.pallas import tpu as pltpu
from jax.sharding import PartitionSpec as P

WINDOW = 1024
rope_base = 500000.0
score_scale = 1.0 / 12.0
masked = -1e30
MESH = pl.DeviceIdType.MESH
TILE = 64
UP = ((2, 4), (4, 1))
ACROSS = ((4, 4), (4, 1))


def tables(rows, n, width):
    half = width // 2
    frequency = rope_base ** (-2.0 * np.arange(half) / width)
    at = np.concatenate([np.arange(rows), rows * np.arange(-(-n // 8) * 8)])
    angles = at[:, None] * frequency
    cos = np.concatenate([np.cos(angles)] * 2, axis=-1)
    sin = np.concatenate([-np.sin(angles), np.sin(angles)], axis=-1)
    return np.stack([cos, sin]).astype(np.float32)


def body(
    n, n_dp, reach, lengths_hbm, q_hbm, k_hbm, v_hbm, tab_hbm, out, z_out,
    lengths, tab, turn, q_raw, raw, stage, spread, q_rot, kv, scores, weights, tops, shares, bias,
    mine, parts_seq, mine2, parts_dp, told, news,
    load_sem, z_send, z_recv, d_send, d_recv, x_sem, s_sem, p_sem, t_sem,
):
    rows, heads, width = k_hbm.shape
    q_heads = q_hbm.shape[1]
    group = q_heads // heads
    tall = group * rows
    hops = reach // 2
    me = lax.axis_index("seq")
    dp = lax.axis_index("dp")
    core = lax.rem(me, 2)
    chip = me // 2
    other = me + 1 - 2 * core
    above = me + 2
    has_above = above < n
    first = core == 0
    second = core == 1
    blocks = jnp.minimum(me, reach) + 1

    loads = [
        pltpu.make_async_copy(k_hbm, raw.at[0], load_sem.at[0]),
        pltpu.make_async_copy(tab_hbm, tab, load_sem.at[3]),
        pltpu.make_async_copy(v_hbm, raw.at[1], load_sem.at[1]),
        pltpu.make_async_copy(q_hbm, q_raw, load_sem.at[2]),
        pltpu.make_async_copy(lengths_hbm, lengths, load_sem.at[4]),
    ]
    for load in loads[:2]:
        load.start()

    barrier = pltpu.get_barrier_semaphore()

    def greet(axis, at):
        pl.semaphore_signal(barrier, inc=1, device_id={axis: at}, device_id_type=MESH)

    def each(low_i, high_i, do):
        def step(i, _):
            do(i)
            return 0

        lax.fori_loop(low_i, high_i, step, 0)

    has_below = me >= 2
    far = me >= 3
    lead = me == 0
    greet("seq", other)
    pl.when(has_above)(lambda: greet("seq", above))
    pl.when(has_below)(lambda: greet("seq", me - 2))

    @pl.when(lead)
    def _():
        each(3, n, lambda j: greet("seq", j))
        each(1, n_dp, lambda j: greet("dp", lax.rem(dp + j, n_dp)))

    greeted = 1 + has_above.astype(jnp.int32) + has_below.astype(jnp.int32) + far.astype(jnp.int32)
    greeted = greeted + lead.astype(jnp.int32) * (n_dp - 1)

    def places(sizes):
        counts = [[heads // size for size in row] for row in sizes]
        flat = [0] + list(np.cumsum(sum(counts, [])))
        return [[int(flat[kind * hops + j]) for j in range(hops)] for kind in range(2)]

    up_at, across_at = places(UP), places(ACROSS)

    def remote(src, dst, send, recv, axis, at):
        return pltpu.make_async_remote_copy(
            src_ref=src, dst_ref=dst, send_sem=send, recv_sem=recv, device_id={axis: at}, device_id_type=MESH
        )

    def some(kind, d, i, size):
        return kv.at[kind, d, pl.ds(i * size, size)]

    def up(kind, hop, i, size=None):
        size = size or UP[kind][hop]
        return remote(
            some(kind, 2 * hop, i, size), some(kind, 2 * hop + 2, i, size),
            z_send.at[kind * hops + hop], z_recv.at[up_at[kind][hop] + i], "seq", above,
        )

    def across(side, kind, hop, i, size=None):
        slot = hop - side
        size = size or ACROSS[kind][slot]
        return remote(
            some(kind, 2 * hop, i, size), some(kind, 2 * hop + 1 - 2 * side, i, size),
            d_send.at[kind * hops + slot], d_recv.at[across_at[kind][slot] + i], "seq", other,
        )

    def extra_up():
        return remote(
            some(1, 1, heads - 1, 1), some(1, 3, heads - 1, 1), x_sem.at[0], x_sem.at[1], "seq", above
        )

    def extra_across():
        return remote(
            some(1, 3, heads - 1, 1), some(1, 4, heads - 1, 1), x_sem.at[2], x_sem.at[3], "seq", other
        )

    half = heads // 2

    def pieces(i, size):
        return i * (half // size), (i + 1) * (half // size)

    def take_up(kind, hop, i):
        each(*pieces(i, UP[kind][hop]), lambda j: up(kind, hop, j).wait_recv())

    def take_across(kind, slot, i):
        size = ACROSS[kind][slot]

        def one(j):
            remote(
                some(kind, 0, j, size), some(kind, 2 * slot + 1, j, size),
                d_send.at[kind * hops + slot], d_recv.at[across_at[kind][slot] + j], "seq", other,
            ).wait_recv()

        each(*pieces(i, size), one)

    def pass_across(side, kind, hop, i):
        each(*pieces(i, ACROSS[kind][hop - side]), lambda j: across(side, kind, hop, j).start())

    def pass_up(kind, hop, i, short=0):
        a, b = pieces(i, UP[kind][hop])
        each(a, b - short, lambda j: up(kind, hop, j).start())

    loads[0].wait()
    for load in loads[2:]:
        load.start()
    loads[1].wait()
    cos_b = tab[0, pl.ds(rows + me, 1), :]
    sin_b = tab[1, pl.ds(rows + me, 1), :]
    turn[0] = tab[0, 0:rows, :] * cos_b - tab[1, 0:rows, :] * sin_b
    turn[1] = tab[1, 0:rows, :] * cos_b + tab[0, 0:rows, :] * sin_b
    stage[0 : rows * heads, :] = raw[0].astype(jnp.float32).reshape(rows * heads, width)

    def turn_k(h):
        x = stage[pl.ds(h, rows, stride=heads), :]
        kv[0, 0, h] = (x * turn[0] + pltpu.roll(x, width // 2, 1) * turn[1]).astype(jnp.bfloat16)

    wide = UP[0][0]

    def turn_ks(i):
        for j in range(wide):
            turn_k(i * wide + j)

    turn_ks(0)
    pl.semaphore_wait(barrier, greeted)

    def first_k(i):
        @pl.when((i + 1) * wide < heads)
        def _():
            turn_ks(i + 1)

        @pl.when(has_above)
        def _():
            up(0, 0, i).start()

    each(0, heads // wide, first_k)

    @pl.when(first)
    def _():
        for i in range(2):
            pass_across(0, 0, 0, i)

    loads[4].wait()
    row_at = me * rows + lax.broadcasted_iota(jnp.int32, (rows, rows), 0)
    start = jnp.zeros((rows, rows), jnp.int32)
    end = jnp.int32(0)
    for i in range(lengths.shape[1]):
        end = end + lengths[0, i]
        start = jnp.where(end <= row_at, end, start)
    low = jnp.maximum(start, row_at - (WINDOW - 1)) - me * rows
    query_at = lax.broadcasted_iota(jnp.int32, (rows, rows), 0)
    for d in range(reach + 1):
        key_at = lax.broadcasted_iota(jnp.int32, (rows, rows), 1) - d * rows
        bias[d] = jnp.where((key_at >= low) & (key_at <= query_at), 0.0, masked)

    loads[3].wait()
    stage[...] = q_raw[...].astype(jnp.float32).reshape(rows * q_heads, width)
    scale = score_scale * math.log2(math.e)

    def turn_q(h):
        for g in range(group):
            x = stage[pl.ds(h * group + g, rows, stride=q_heads), :]
            turned = x * turn[0] + pltpu.roll(x, width // 2, 1) * turn[1]
            q_rot[h, g * rows : (g + 1) * rows, :] = (turned * scale).astype(jnp.bfloat16)

    each(0, heads, turn_q)

    loads[2].wait()
    stage[0 : rows * heads, :] = raw[1].astype(jnp.float32).reshape(rows * heads, width)

    def move_v(h):
        kv[1, 0, h] = stage[pl.ds(h, rows, stride=heads), :].astype(jnp.bfloat16)

    each(0, heads, move_v)

    @pl.when(first)
    def _():
        for i in range(2):
            pass_across(0, 1, 0, i)

    def score(d, h, fresh=False):
        s = lax.dot_general(
            q_rot[h], kv[0, d, h], (((1,), (1,)), ((), ())), preferred_element_type=jnp.float32
        )
        for g in range(group):
            part = slice(g * rows, (g + 1) * rows)
            t = s[part] + bias[d]
            scores[h, d, part, :] = t
            top = functools.reduce(jnp.maximum, [t[:, i * width : (i + 1) * width] for i in range(rows // width)])
            tops[h, part, :] = top if fresh else jnp.maximum(tops[h, part, :], top)

    def scores_of(d, i):
        each(i * half, (i + 1) * half, lambda h: score(d, h))

    each(0, heads, lambda h: score(0, h, fresh=True))

    @pl.when(second)
    def _():
        def step(i):
            take_across(0, 0, i)
            scores_of(1, i)

        for i in range(2):
            step(i)

    @pl.when(chip >= 1)
    def _():
        for i in range(2):
            take_up(0, 0, i)
            pl.when(has_above)(functools.partial(pass_up, 0, 1, i))
            pl.when(first)(functools.partial(pass_across, 0, 0, 1, i))
            pl.when(second)(functools.partial(pass_across, 1, 0, 1, i))
            scores_of(2, i)

    @pl.when(has_above)
    def _():
        for i in range(2):
            pass_up(1, 0, i)

    @pl.when(chip >= 1)
    def _():
        for i in range(2):
            pl.when(first)(functools.partial(take_across, 0, 0, i))
            pl.when(second)(functools.partial(take_across, 0, 1, i))
            scores_of(1 + 2 * core, i)

    @pl.when(chip >= 2)
    def _():
        for i in range(2):
            take_up(0, 1, i)
            pl.when(second)(functools.partial(pass_across, 1, 0, 2, i))
            scores_of(4, i)

        @pl.when(first)
        def _():
            for i in range(2):
                take_across(0, 1, i)
                scores_of(3, i)

    def finish(h, square, peak, total, part):
        shares[h, part, :] = jnp.broadcast_to(1.0 / total, (total.shape[0], width))
        lse = peak * math.log(2.0) + jnp.log(total)
        return square + jnp.sum(lse * lse, axis=0, keepdims=True)

    def weigh(h, square):
        for i in range(tall // TILE):
            part = slice(i * TILE, (i + 1) * TILE)
            peak = jnp.max(tops[h, part, :], axis=1, keepdims=True)
            total = jnp.zeros((TILE, width), jnp.float32)
            for d in range(reach + 1):
                p = jnp.exp2(scores[h, d, part, :] - peak)
                weights[h, d, part, :] = p.astype(jnp.bfloat16)
                for c in range(rows // width):
                    total = total + p[:, c * width : (c + 1) * width]
            square = finish(h, square, peak, jnp.sum(total, axis=1, keepdims=True), part)
        return square

    def weigh_some(h, square):
        for i in range(tall // TILE):
            part = slice(i * TILE, (i + 1) * TILE)
            peak = jnp.max(tops[h, part, :], axis=1, keepdims=True)

            def step(d, total):
                p = jnp.exp2(scores[h, d, part, :] - peak)
                weights[h, d, part, :] = p.astype(jnp.bfloat16)
                for c in range(rows // width):
                    total = total + p[:, c * width : (c + 1) * width]
                return total

            total = lax.fori_loop(0, blocks, step, jnp.zeros((TILE, width), jnp.float32))
            square = finish(h, square, peak, jnp.sum(total, axis=1, keepdims=True), part)
        return square

    def settle(square):
        mine[...] = jnp.broadcast_to(square, mine.shape)

    @pl.when(chip >= 2)
    def _():
        settle(lax.fori_loop(0, heads, weigh, jnp.zeros((1, 1), jnp.float32)))

    @pl.when(chip < 2)
    def _():
        settle(lax.fori_loop(0, heads, weigh_some, jnp.zeros((1, 1), jnp.float32)))

    def report(j):
        return remote(mine, parts_seq.at[j], s_sem.at[0], s_sem.at[1], "seq", 0)

    def tell_dp(j):
        return remote(mine2, parts_dp.at[dp], p_sem.at[0], p_sem.at[1], "dp", lax.rem(dp + j, n_dp))

    def tell(j):
        return remote(told, news, t_sem.at[0], t_sem.at[1], "seq", j)

    @pl.when(me > 0)
    def _():
        report(me).start()

    @pl.when(chip >= 1)
    def _():
        for i in range(2):
            take_up(1, 0, i)

            @pl.when(first)
            def _(i=i):
                pass_across(0, 1, 1, i)
                if i == 1:
                    for j in range(2):
                        take_across(1, 0, j)

                @pl.when(has_above)
                def _():
                    if i == 1:
                        extra_up().start()
                    pass_up(1, 1, i)

            @pl.when(second)
            def _(i=i):
                pass_across(1, 1, 1, i)
                pl.when(has_above)(functools.partial(pass_up, 1, 1, i, short=i))

    @pl.when(second)
    def _():
        for i in range(2):
            take_across(1, 0, i)

        @pl.when(chip >= 1)
        def _():
            for i in range(2):
                take_across(1, 1, i)

    def give(h, o):
        o = o * shares[h]
        for g in range(group):
            spread[pl.ds(h * group + g, rows, stride=q_heads), :] = o[g * rows : (g + 1) * rows]

    def blend(h, which):
        w = jnp.concatenate([weights[h, d] for d in which], axis=1)
        v = jnp.concatenate([kv[1, d, h] for d in which], axis=0)
        return jnp.dot(w, v, preferred_element_type=jnp.float32)

    def mix(h):
        up(1, 1, h).wait_recv()

        @pl.when(second)
        def _():
            across(1, 1, 2, h).start()

        @pl.when(first)
        def _():
            across(0, 1, 1, h).wait_recv()

        give(h, blend(h, range(reach + 1)))

    last = heads - 1

    @pl.when(chip >= 2)
    def _():
        each(0, half, mix)

        @pl.when(first)
        def _():
            extra_up().wait_recv()
            extra_across().start()

        each(half, last, mix)
        tops[last] = blend(last, range(reach))

    @pl.when(chip < 2)
    def _():
        def mix_some(h):
            def step(d, o):
                return o + jnp.dot(weights[h, d], kv[1, d, h], preferred_element_type=jnp.float32)

            give(h, lax.fori_loop(0, blocks, step, jnp.zeros((tall, width), jnp.float32)))

        each(0, heads, mix_some)

    @pl.when(lead)
    def _():
        parts_seq[0] = mine[...]
        others, peers = parts_seq.at[pl.ds(1, n - 1)], parts_dp.at[pl.ds(1, n_dp - 1)]
        remote(others, others, s_sem.at[0], s_sem.at[1], "seq", other).wait_recv()
        column = jnp.sum(parts_seq[...], axis=0)
        mine2[...] = column
        parts_dp[dp] = column
        each(1, n_dp, lambda j: tell_dp(j).start())
        remote(peers, peers, p_sem.at[0], p_sem.at[1], "seq", other).wait_recv()
        whole = jnp.sum(parts_dp[...], axis=0) / (n_dp * n * rows * q_heads)
        told[...] = whole
        news[...] = whole
        each(1, n, lambda j: tell(j).start())
        remote(peers, peers, p_sem.at[0], p_sem.at[1], "seq", other).wait_send()
        remote(others, others, t_sem.at[0], t_sem.at[1], "seq", other).wait_send()

    @pl.when(me > 0)
    def _():
        tell(me).wait_recv()

    z_out[...] = news[...]

    def sent_up(kind, hop, count=heads):
        up(kind, hop, 0, count).wait_send()

    def sent_across(side, kind, hop, count=heads):
        across(side, kind, hop, 0, count).wait_send()

    for kind in range(2):
        pl.when(has_above)(functools.partial(sent_up, kind, 0))
        pl.when(first)(functools.partial(sent_across, 0, kind, 0))
        pl.when(first & (chip >= 1))(functools.partial(sent_across, 0, kind, 1))
        pl.when(second & (chip >= 1))(functools.partial(sent_across, 1, kind, 1))
    pl.when(has_above & (chip >= 1))(functools.partial(sent_up, 0, 1))
    pl.when(second & (chip >= 2))(functools.partial(sent_across, 1, 0, 2))

    @pl.when(me > 0)
    def _():
        report(me).wait_send()

    @pl.when(chip >= 2)
    def _():
        @pl.when(first)
        def _():
            up(1, 1, last).wait_recv()

        @pl.when(second)
        def _():
            extra_across().wait_recv()

        give(last, tops[last] + blend(last, [reach]))

    out[...] = spread[...].reshape(rows, q_heads, width).astype(jnp.bfloat16)

    @pl.when(chip >= 1)
    def _():
        @pl.when(first & has_above)
        def _():
            sent_up(1, 1)
            extra_up().wait_send()

        pl.when(second & has_above)(functools.partial(sent_up, 1, 1, last))

    @pl.when(chip >= 2)
    def _():
        pl.when(first)(lambda: extra_across().wait_send())
        pl.when(second)(functools.partial(sent_across, 1, 1, 2, last))


def place(held, z_held, out, z_out, z_one, sem):
    copies = [
        pltpu.make_async_copy(held, out, sem.at[0]),
        pltpu.make_async_copy(z_one, z_out, sem.at[1]),
    ]
    copies[0].start()
    z_one[...] = z_held[0:1, 0:1]
    copies[1].start()
    for copy in copies:
        copy.wait()


def shards(queries, keys, values, lengths):
    _, rows, q_heads, width = queries.shape
    heads = keys.shape[2]
    group = q_heads // heads
    n = lax.axis_size("seq")
    n_dp = lax.axis_size("dp")
    reach = -(-(WINDOW - 1) // rows)
    assert n % 2 == 0 and reach == 4 and heads % 8 == 0
    hops = reach // 2
    tab = jnp.asarray(tables(rows, n, width))
    vmem = pl.BlockSpec(memory_space=pltpu.VMEM)
    anywhere = pl.BlockSpec(memory_space=pl.ANY)
    dma = pltpu.SemaphoreType.DMA
    out, z = pl.pallas_call(
        functools.partial(body, n, n_dp, reach),
        out_shape=(
            pltpu.VMEM((rows, q_heads, width), jnp.bfloat16),
            pltpu.VMEM((8, width), jnp.float32),
        ),
        in_specs=[anywhere] * 5,
        out_specs=(vmem, vmem),
        scratch_shapes=[
            pltpu.SMEM(lengths.shape, jnp.int32),
            pltpu.VMEM(tab.shape, jnp.float32),
            pltpu.VMEM((2, rows, width), jnp.float32),
            pltpu.VMEM((rows, q_heads, width), jnp.bfloat16),
            pltpu.VMEM((2, rows, heads, width), jnp.bfloat16),
            pltpu.VMEM((rows * q_heads, width), jnp.float32),
            pltpu.VMEM((rows * q_heads, width), jnp.float32),
            pltpu.VMEM((heads, group * rows, width), jnp.bfloat16),
            pltpu.VMEM((2, reach + 1, heads, rows, width), jnp.bfloat16),
            pltpu.VMEM((heads, reach + 1, group * rows, rows), jnp.float32),
            pltpu.VMEM((heads, reach + 1, group * rows, rows), jnp.bfloat16),
            pltpu.VMEM((heads, group * rows, width), jnp.float32),
            pltpu.VMEM((heads, group * rows, width), jnp.float32),
            pltpu.VMEM((reach + 1, rows, rows), jnp.float32),
            pltpu.VMEM((8, width), jnp.float32),
            pltpu.VMEM((n, 8, width), jnp.float32),
            pltpu.VMEM((8, width), jnp.float32),
            pltpu.VMEM((n_dp, 8, width), jnp.float32),
            pltpu.VMEM((8, width), jnp.float32),
            pltpu.VMEM((8, width), jnp.float32),
            dma((5,)),
            dma((2 * hops,)),
            dma((sum(heads // size for row in UP for size in row),)),
            dma((2 * hops,)),
            dma((sum(heads // size for row in ACROSS for size in row),)),
            dma((4,)),
            dma((2,)),
            dma((2,)),
            dma((2,)),
        ],
        compiler_params=pltpu.CompilerParams(
            collective_id=0, has_side_effects=True, vmem_limit_bytes=56 * 1024 * 1024
        ),
        name="attend",
    )(lengths, queries[0], keys[0], values[0], tab)
    out, z = pl.pallas_call(
        place,
        out_shape=(
            jax.ShapeDtypeStruct((rows, q_heads, width), jnp.bfloat16),
            jax.ShapeDtypeStruct((1, 1), jnp.float32),
        ),
        in_specs=[vmem, vmem],
        out_specs=(anywhere, anywhere),
        scratch_shapes=[pltpu.VMEM((1, 1), jnp.float32), dma((2,))],
        compiler_params=pltpu.CompilerParams(vmem_limit_bytes=4 * 1024 * 1024),
        name="place",
    )(out, z)
    return out[None], z[0, 0]


def solution(mesh):
    placed = (
        P("dp", "seq", None, None),
        P("dp", "seq", None, None),
        P("dp", "seq", None, None),
        P("dp", None),
    )
    return jax.shard_map(
        shards,
        mesh=mesh,
        in_specs=placed,
        out_specs=(P("dp", "seq", None, None), P()),
        check_vma=False,
    )
```

time: 53.6 us -> 50.6 us (0.944)
  between operations: 2.33 us -> 0.64 us
  local copies, waits for them, and re-layouts: 0.97 us -> 0 us
    pallas_call x1, Pallas kernels: 50.2 us -> 48.9 us  [shards(): pl.pallas_call(functools.partial(body, n, n_dp, reach), out_shape=(pltpu....]
    pallas_call x0 -> x1, Pallas kernels: none -> 0.99 us  [shards(): pl.pallas_call(place, out_shape=(jax.ShapeDtypeStruct((rows, q_heads, wid...]
    unnamed x1 -> x0, local copies, waits for them, and re-layouts: 0.97 us -> none
where the time goes in v2:
time: 50.6 us; the launch traced here: 50.5 us
  Pallas kernels  49.8 us (98%)
  between operations  0.64 us (1%)
    pallas_call x1, Pallas kernels, shards(): pl.pallas_call(functools.partial(body, n, n_dp, reach), out_shape=(pltpu....  48.9 us

profile of v2, /device:TPU:16, one launch (start us, length us, event | category | flops | bytes accessed | tf_op | source)
XLA Modules:
  0.0 50.5 jit_solution(18397374747583571644)
XLA Ops:
  0.6 48.9 %attend.1 = (bf16[256,16,128]{2,1,0:T(8,128)(2,1)S(1)}, f32[8,128]{1,0:T(8,128)S(1)}) custom-call(s32[1,8]{1,0:T(1,128)} %lengths_hbm.1, bf16[256,16,128]{2,1,0:T(8,128)(2,1)} %bitcast.5, bf16[256,8,128]{2,1,0:T(8,128)(2,1)} %bitcast.6, bf16[256,8,128]{2,1,0:T(8,128)(2,1)} %bitcast.7, f32[2,264,128]{2,1,0:T(8,128)} %constant.2.clone.tab_hbm), custom_call_target="tpu_custom_call" | custom-call | tf_op jit(solution)/shard_map/attend/pallas_call | solution.py:526
  49.5 1.0 %place.1 = (bf16[256,16,128]{2,1,0:T(8,128)(2,1)}, f32[1,1]{1,0:T(1,128)}) custom-call(bf16[256,16,128]{2,1,0:T(8,128)(2,1)S(1)} %get-tuple-element.6.held, f32[8,128]{1,0:T(8,128)S(1)} %get-tuple-element.7.z_held), custom_call_target="tpu_custom_call" | custom-call | tf_op jit(solution)/shard_map/place/pallas_call | solution.py:570

commit v3 on v2

--- a/solution.py
+++ b/solution.py
@@ -15,8 +15,8 @@
 masked = -1e30
 MESH = pl.DeviceIdType.MESH
 TILE = 64
-UP = ((2, 4), (4, 1))
-ACROSS = ((4, 4), (4, 1))
+UP = (((2, 2, 2, 2), (4, 4)), ((4, 4), (4, 1, 1, 1)))
+ACROSS = (((4, 4), (4, 4)), ((4, 4), (4, 1, 1, 1, 1)))
 
 
 def tables(rows, n, width):
@@ -31,9 +31,9 @@
 
 def body(
     n, n_dp, reach, lengths_hbm, q_hbm, k_hbm, v_hbm, tab_hbm, out, z_out,
-    lengths, tab, turn, q_raw, raw, stage, spread, q_rot, kv, scores, weights, tops, shares, bias,
+    lengths, tab, turn, q_raw, lead_raw, raw, stage, spread, q_rot, kv, scores, weights, tops, shares, bias,
     mine, parts_seq, mine2, parts_dp, told, news,
-    load_sem, z_send, z_recv, d_send, d_recv, x_sem, s_sem, p_sem, t_sem,
+    load_sem, z_send, z_recv, d_send, d_recv, x_recv, s_sem, p_sem, t_sem,
 ):
     rows, heads, width = k_hbm.shape
     q_heads = q_hbm.shape[1]
@@ -51,14 +51,16 @@
     second = core == 1
     blocks = jnp.minimum(me, reach) + 1
 
+    wide = heads // len(UP[0][0])
     loads = [
-        pltpu.make_async_copy(k_hbm, raw.at[0], load_sem.at[0]),
+        pltpu.make_async_copy(k_hbm.at[:, 0:wide], lead_raw.at[:, 0:wide], load_sem.at[0]),
         pltpu.make_async_copy(tab_hbm, tab, load_sem.at[3]),
+        pltpu.make_async_copy(k_hbm, raw.at[0], load_sem.at[5]),
         pltpu.make_async_copy(v_hbm, raw.at[1], load_sem.at[1]),
         pltpu.make_async_copy(q_hbm, q_raw, load_sem.at[2]),
         pltpu.make_async_copy(lengths_hbm, lengths, load_sem.at[4]),
     ]
-    for load in loads[:2]:
+    for load in loads[:3]:
         load.start()
 
     barrier = pltpu.get_barrier_semaphore()
@@ -88,12 +90,19 @@
     greeted = 1 + has_above.astype(jnp.int32) + has_below.astype(jnp.int32) + far.astype(jnp.int32)
     greeted = greeted + lead.astype(jnp.int32) * (n_dp - 1)
 
-    def places(sizes):
-        counts = [[heads // size for size in row] for row in sizes]
-        flat = [0] + list(np.cumsum(sum(counts, [])))
-        return [[int(flat[kind * hops + j]) for j in range(hops)] for kind in range(2)]
-
-    up_at, across_at = places(UP), places(ACROSS)
+    def lay(table):
+        count = 0
+        laid = []
+        for row in table:
+            for eighths in row:
+                at, cuts = 0, []
+                for size in eighths:
+                    cuts.append((count, at * heads // 8, size * heads // 8))
+                    count, at = count + 1, at + size
+                laid.append(cuts)
+        return laid
+
+    up_cuts, across_cuts = lay(UP), lay(ACROSS)
 
     def remote(src, dst, send, recv, axis, at):
         return pltpu.make_async_remote_copy(
@@ -101,75 +110,77 @@
         )
 
     def some(kind, d, i, size):
-        return kv.at[kind, d, pl.ds(i * size, size)]
-
-    def up(kind, hop, i, size=None):
-        size = size or UP[kind][hop]
+        return kv.at[kind, d, pl.ds(i, size)]
+
+    def up(kind, hop, cut):
+        at, start, size = cut
+        late = kind * hop
         return remote(
-            some(kind, 2 * hop, i, size), some(kind, 2 * hop + 2, i, size),
-            z_send.at[kind * hops + hop], z_recv.at[up_at[kind][hop] + i], "seq", above,
+            some(kind, 2 * hop, start, size), some(kind, 2 * hop + 2, start, size),
+            z_send.at[late], z_recv.at[at], "seq", above,
         )
 
-    def across(side, kind, hop, i, size=None):
-        slot = hop - side
-        size = size or ACROSS[kind][slot]
+    def across(side, kind, hop, cut):
+        at, start, size = cut
+        late = int(kind == 1 and hop == 2)
         return remote(
-            some(kind, 2 * hop, i, size), some(kind, 2 * hop + 1 - 2 * side, i, size),
-            d_send.at[kind * hops + slot], d_recv.at[across_at[kind][slot] + i], "seq", other,
+            some(kind, 2 * hop, start, size), some(kind, 2 * hop + 1 - 2 * side, start, size),
+            d_send.at[late], d_recv.at[at], "seq", other,
         )
 
-    def extra_up():
-        return remote(
-            some(1, 1, heads - 1, 1), some(1, 3, heads - 1, 1), x_sem.at[0], x_sem.at[1], "seq", above
-        )
-
-    def extra_across():
-        return remote(
-            some(1, 3, heads - 1, 1), some(1, 4, heads - 1, 1), x_sem.at[2], x_sem.at[3], "seq", other
-        )
+    last = heads - 1
+
+    def lend_up():
+        return remote(some(1, 1, last, 1), some(1, 3, last, 1), z_send.at[1], x_recv.at[0], "seq", above)
+
+    def lend_across():
+        return remote(some(1, 3, last, 1), some(1, 4, last, 1), d_send.at[1], x_recv.at[1], "seq", other)
+
+    def cross_up(j):
+        h = last - 1 + j
+        return remote(some(1, 3, h, 1), some(1, 4, h, 1), z_send.at[1], x_recv.at[2 + j], "seq", me + 1)
 
     half = heads // 2
 
-    def pieces(i, size):
-        return i * (half // size), (i + 1) * (half // size)
+    def cuts_of(cuts, i):
+        return [cut for cut in cuts if i * half <= cut[1] < (i + 1) * half]
 
     def take_up(kind, hop, i):
-        each(*pieces(i, UP[kind][hop]), lambda j: up(kind, hop, j).wait_recv())
+        for cut in cuts_of(up_cuts[kind * hops + hop], i):
+            up(kind, hop, cut).wait_recv()
+
+    def take_cut(kind, slot, cut):
+        at, start, size = cut
+        remote(
+            some(kind, 0, start, size), some(kind, 2 * slot + 1, start, size),
+            d_send.at[0], d_recv.at[at], "seq", other,
+        ).wait_recv()
 
     def take_across(kind, slot, i):
-        size = ACROSS[kind][slot]
-
-        def one(j):
-            remote(
-                some(kind, 0, j, size), some(kind, 2 * slot + 1, j, size),
-                d_send.at[kind * hops + slot], d_recv.at[across_at[kind][slot] + j], "seq", other,
-            ).wait_recv()
-
-        each(*pieces(i, size), one)
+        for cut in cuts_of(across_cuts[kind * hops + slot], i):
+            take_cut(kind, slot, cut)
 
     def pass_across(side, kind, hop, i):
-        each(*pieces(i, ACROSS[kind][hop - side]), lambda j: across(side, kind, hop, j).start())
+        for cut in cuts_of(across_cuts[kind * hops + hop - side], i):
+            across(side, kind, hop, cut).start()
 
     def pass_up(kind, hop, i, short=0):
-        a, b = pieces(i, UP[kind][hop])
-        each(a, b - short, lambda j: up(kind, hop, j).start())
+        cuts = cuts_of(up_cuts[kind * hops + hop], i)
+        for cut in cuts[: len(cuts) - short]:
+            up(kind, hop, cut).start()
 
     loads[0].wait()
-    for load in loads[2:]:
-        load.start()
     loads[1].wait()
     cos_b = tab[0, pl.ds(rows + me, 1), :]
     sin_b = tab[1, pl.ds(rows + me, 1), :]
     turn[0] = tab[0, 0:rows, :] * cos_b - tab[1, 0:rows, :] * sin_b
     turn[1] = tab[1, 0:rows, :] * cos_b + tab[0, 0:rows, :] * sin_b
-    stage[0 : rows * heads, :] = raw[0].astype(jnp.float32).reshape(rows * heads, width)
+    stage[0 : rows * heads, :] = lead_raw[...].astype(jnp.float32).reshape(rows * heads, width)
 
     def turn_k(h):
         x = stage[pl.ds(h, rows, stride=heads), :]
         kv[0, 0, h] = (x * turn[0] + pltpu.roll(x, width // 2, 1) * turn[1]).astype(jnp.bfloat16)
 
-    wide = UP[0][0]
-
     def turn_ks(i):
         for j in range(wide):
             turn_k(i * wide + j)
@@ -177,23 +188,26 @@
     turn_ks(0)
     pl.semaphore_wait(barrier, greeted)
 
-    def first_k(i):
-        @pl.when((i + 1) * wide < heads)
-        def _():
+    def send_k(i):
+        pl.when(has_above)(lambda: up(0, 0, up_cuts[0][i]).start())
+
+    send_k(0)
+    loads[2].wait()
+    for load in loads[3:]:
+        load.start()
+    stage[0 : rows * heads, :] = raw[0].astype(jnp.float32).reshape(rows * heads, width)
+    turn_ks(1)
+    for i in range(1, len(up_cuts[0])):
+        if i + 1 < len(up_cuts[0]):
             turn_ks(i + 1)
-
-        @pl.when(has_above)
-        def _():
-            up(0, 0, i).start()
-
-    each(0, heads // wide, first_k)
+        send_k(i)
 
     @pl.when(first)
     def _():
         for i in range(2):
             pass_across(0, 0, 0, i)
 
-    loads[4].wait()
+    loads[5].wait()
     row_at = me * rows + lax.broadcasted_iota(jnp.int32, (rows, rows), 0)
     start = jnp.zeros((rows, rows), jnp.int32)
     end = jnp.int32(0)
@@ -206,7 +220,7 @@
         key_at = lax.broadcasted_iota(jnp.int32, (rows, rows), 1) - d * rows
         bias[d] = jnp.where((key_at >= low) & (key_at <= query_at), 0.0, masked)
 
-    loads[3].wait()
+    loads[4].wait()
     stage[...] = q_raw[...].astype(jnp.float32).reshape(rows * q_heads, width)
     scale = score_scale * math.log2(math.e)
 
@@ -218,7 +232,7 @@
 
     each(0, heads, turn_q)
 
-    loads[2].wait()
+    loads[3].wait()
     stage[0 : rows * heads, :] = raw[1].astype(jnp.float32).reshape(rows * heads, width)
 
     def move_v(h):
@@ -359,17 +373,13 @@
                 if i == 1:
                     for j in range(2):
                         take_across(1, 0, j)
-
-                @pl.when(has_above)
-                def _():
-                    if i == 1:
-                        extra_up().start()
-                    pass_up(1, 1, i)
+                    pl.when(has_above)(lambda: lend_up().start())
+                pl.when(has_above)(functools.partial(pass_up, 1, 1, i, short=i))
 
             @pl.when(second)
             def _(i=i):
+                pl.when(has_above)(functools.partial(pass_up, 1, 1, i))
                 pass_across(1, 1, 1, i)
-                pl.when(has_above)(functools.partial(pass_up, 1, 1, i, short=i))
 
     @pl.when(second)
     def _():
@@ -381,6 +391,11 @@
             for i in range(2):
                 take_across(1, 1, i)
 
+            @pl.when(has_above)
+            def _():
+                for j in range(2):
+                    cross_up(j).start()
+
     def give(h, o):
         o = o * shares[h]
         for g in range(group):
@@ -392,31 +407,42 @@
         return jnp.dot(w, v, preferred_element_type=jnp.float32)
 
     def mix(h):
-        up(1, 1, h).wait_recv()
+        give(h, tops[h] + blend(h, (reach - 1, reach)))
+
+    def mix_early(h):
+        tops[h] = blend(h, range(reach - 1))
+
+    @pl.when(chip >= 2)
+    def _():
+        each(0, heads, mix_early)
+        ups, acrosses = up_cuts[-1], across_cuts[-1]
+
+        def mixed(cut):
+            each(cut[1], cut[1] + cut[2], mix)
+
+        @pl.when(first)
+        def _():
+            for j in range(2):
+                up(1, 1, ups[j]).wait_recv()
+                take_cut(1, 1, acrosses[j])
+                mixed(ups[j])
+                if j == 0:
+                    lend_up().wait_recv()
+                    lend_across().start()
+
+            cross_up(0).wait_recv()
+            take_cut(1, 1, acrosses[3])
+            mixed(ups[3])
+            up(1, 1, ups[2]).wait_recv()
+            take_cut(1, 1, acrosses[2])
+            mixed(ups[2])
 
         @pl.when(second)
         def _():
-            across(1, 1, 2, h).start()
-
-        @pl.when(first)
-        def _():
-            across(0, 1, 1, h).wait_recv()
-
-        give(h, blend(h, range(reach + 1)))
-
-    last = heads - 1
-
-    @pl.when(chip >= 2)
-    def _():
-        each(0, half, mix)
-
-        @pl.when(first)
-        def _():
-            extra_up().wait_recv()
-            extra_across().start()
-
-        each(half, last, mix)
-        tops[last] = blend(last, range(reach))
+            for j in range(4):
+                up(1, 1, ups[j]).wait_recv()
+                across(1, 1, 2, acrosses[j]).start()
+                mixed(ups[j])
 
     @pl.when(chip < 2)
     def _():
@@ -451,19 +477,15 @@
 
     z_out[...] = news[...]
 
-    def sent_up(kind, hop, count=heads):
-        up(kind, hop, 0, count).wait_send()
-
-    def sent_across(side, kind, hop, count=heads):
-        across(side, kind, hop, 0, count).wait_send()
-
-    for kind in range(2):
-        pl.when(has_above)(functools.partial(sent_up, kind, 0))
-        pl.when(first)(functools.partial(sent_across, 0, kind, 0))
-        pl.when(first & (chip >= 1))(functools.partial(sent_across, 0, kind, 1))
-        pl.when(second & (chip >= 1))(functools.partial(sent_across, 1, kind, 1))
-    pl.when(has_above & (chip >= 1))(functools.partial(sent_up, 0, 1))
-    pl.when(second & (chip >= 2))(functools.partial(sent_across, 1, 0, 2))
+    def sent(view, sem):
+        remote(view, view, sem, sem, "seq", other).wait_send()
+
+    pl.when(has_above & (chip == 0))(lambda: sent(kv.at[0, 0:2], z_send.at[0]))
+    pl.when(has_above & (chip >= 1))(lambda: sent(kv.at[0, 0:3], z_send.at[0]))
+    pl.when(first & (chip == 0))(lambda: sent(kv.at[0, 0:2], d_send.at[0]))
+    pl.when(first & (chip >= 1))(lambda: sent(kv.at[0, 0:4], d_send.at[0]))
+    pl.when(second & (chip == 1))(lambda: sent(kv.at[0, 0:2], d_send.at[0]))
+    pl.when(second & (chip >= 2))(lambda: sent(kv.at[0, 0:3], d_send.at[0]))
 
     @pl.when(me > 0)
     def _():
@@ -473,29 +495,20 @@
     def _():
         @pl.when(first)
         def _():
-            up(1, 1, last).wait_recv()
+            cross_up(1).wait_recv()
+            mix(last)
 
         @pl.when(second)
         def _():
-            extra_across().wait_recv()
-
-        give(last, tops[last] + blend(last, [reach]))
+            lend_across().wait_recv()
+            mix(last)
 
     out[...] = spread[...].reshape(rows, q_heads, width).astype(jnp.bfloat16)
 
-    @pl.when(chip >= 1)
-    def _():
-        @pl.when(first & has_above)
-        def _():
-            sent_up(1, 1)
-            extra_up().wait_send()
-
-        pl.when(second & has_above)(functools.partial(sent_up, 1, 1, last))
-
-    @pl.when(chip >= 2)
-    def _():
-        pl.when(first)(lambda: extra_across().wait_send())
-        pl.when(second)(functools.partial(sent_across, 1, 1, 2, last))
+    pl.when(first & has_above & (chip >= 1))(lambda: sent(kv.at[1, 0, 0:last], z_send.at[1]))
+    pl.when(second & has_above & (chip >= 1))(lambda: sent(kv.at[1, 0:3, 0 : (heads + 1) // 3], z_send.at[1]))
+    pl.when(first & (chip >= 2))(lambda: sent(kv.at[1, 0, 0:1], d_send.at[1]))
+    pl.when(second & (chip >= 2))(lambda: sent(kv.at[1, 0, 0:last], d_send.at[1]))
 
 
 def place(held, z_held, out, z_out, z_one, sem):
@@ -517,7 +530,7 @@
     n = lax.axis_size("seq")
     n_dp = lax.axis_size("dp")
     reach = -(-(WINDOW - 1) // rows)
-    assert n % 2 == 0 and reach == 4 and heads % 8 == 0
+    assert n % 2 == 0 and reach == 4 and heads == 8
     hops = reach // 2
     tab = jnp.asarray(tables(rows, n, width))
     vmem = pl.BlockSpec(memory_space=pltpu.VMEM)
@@ -536,6 +549,7 @@
             pltpu.VMEM(tab.shape, jnp.float32),
             pltpu.VMEM((2, rows, width), jnp.float32),
             pltpu.VMEM((rows, q_heads, width), jnp.bfloat16),
+            pltpu.VMEM((rows, heads, width), jnp.bfloat16),
             pltpu.VMEM((2, rows, heads, width), jnp.bfloat16),
             pltpu.VMEM((rows * q_heads, width), jnp.float32),
             pltpu.VMEM((rows * q_heads, width), jnp.float32),
@@ -552,11 +566,11 @@
             pltpu.VMEM((n_dp, 8, width), jnp.float32),
             pltpu.VMEM((8, width), jnp.float32),
             pltpu.VMEM((8, width), jnp.float32),
-            dma((5,)),
-            dma((2 * hops,)),
-            dma((sum(heads // size for row in UP for size in row),)),
-            dma((2 * hops,)),
-            dma((sum(heads // size for row in ACROSS for size in row),)),
+            dma((6,)),
+            dma((2,)),
+            dma((sum(len(cuts) for row in UP for cuts in row),)),
+            dma((2,)),
+            dma((sum(len(cuts) for row in ACROSS for cuts in row),)),
             dma((4,)),
             dma((2,)),
             dma((2,)),

time: 50.6 us -> 50.3 us (level)
  no operation moved by 1% of the time
where the time goes in v3:
time: 50.3 us; the launch traced here: 50.1 us
  Pallas kernels  49.5 us (98%)
  between operations  0.64 us (1%)
    pallas_call x1, Pallas kernels, shards(): pl.pallas_call(functools.partial(body, n, n_dp, reach), out_shape=(pltpu....  48.5 us

profile of v3, /device:TPU:16, one launch (start us, length us, event | category | flops | bytes accessed | tf_op | source)
XLA Modules:
  0.0 50.1 jit_solution(15302266794438948263)
XLA Ops:
  0.6 48.5 %attend.1 = (bf16[256,16,128]{2,1,0:T(8,128)(2,1)S(1)}, f32[8,128]{1,0:T(8,128)S(1)}) custom-call(s32[1,8]{1,0:T(1,128)} %lengths_hbm.1, bf16[256,16,128]{2,1,0:T(8,128)(2,1)} %bitcast.5, bf16[256,8,128]{2,1,0:T(8,128)(2,1)} %bitcast.6, bf16[256,8,128]{2,1,0:T(8,128)(2,1)} %bitcast.7, f32[2,264,128]{2,1,0:T(8,128)} %constant.2.clone.tab_hbm), custom_call_target="tpu_custom_call" | custom-call | tf_op jit(solution)/shard_map/attend/pallas_call | solution.py:539
  49.1 1.0 %place.1 = (bf16[256,16,128]{2,1,0:T(8,128)(2,1)}, f32[1,1]{1,0:T(1,128)}) custom-call(bf16[256,16,128]{2,1,0:T(8,128)(2,1)S(1)} %get-tuple-element.6.held, f32[8,128]{1,0:T(8,128)S(1)} %get-tuple-element.7.z_held), custom_call_target="tpu_custom_call" | custom-call | tf_op jit(solution)/shard_map/place/pallas_call | solution.py:584

commit v4 on v3

--- a/solution.py
+++ b/solution.py
@@ -15,6 +15,7 @@
 masked = -1e30
 MESH = pl.DeviceIdType.MESH
 TILE = 64
+PARTS = 4
 UP = (((2, 2, 2, 2), (4, 4)), ((4, 4), (4, 1, 1, 1)))
 ACROSS = (((4, 4), (4, 4)), ((4, 4), (4, 1, 1, 1, 1)))
 
@@ -30,10 +31,10 @@
 
 
 def body(
-    n, n_dp, reach, lengths_hbm, q_hbm, k_hbm, v_hbm, tab_hbm, out, z_out,
-    lengths, tab, turn, q_raw, lead_raw, raw, stage, spread, q_rot, kv, scores, weights, tops, shares, bias,
+    n, n_dp, reach, lengths_hbm, q_hbm, k_hbm, v_hbm, tab_hbm, spread, z_out,
+    lengths, tab, turn, q_raw, lead_raw, raw, stage, q_rot, kv, scores, weights, tops, shares, bias,
     mine, parts_seq, mine2, parts_dp, told, news,
-    load_sem, z_send, z_recv, d_send, d_recv, x_recv, s_sem, p_sem, t_sem,
+    load_sem, z_send, z_recv, d_send, d_recv, x_recv, s_sem, p_sem,
 ):
     rows, heads, width = k_hbm.shape
     q_heads = q_hbm.shape[1]
@@ -54,11 +55,11 @@
     wide = heads // len(UP[0][0])
     loads = [
         pltpu.make_async_copy(k_hbm.at[:, 0:wide], lead_raw.at[:, 0:wide], load_sem.at[0]),
-        pltpu.make_async_copy(tab_hbm, tab, load_sem.at[3]),
-        pltpu.make_async_copy(k_hbm, raw.at[0], load_sem.at[5]),
-        pltpu.make_async_copy(v_hbm, raw.at[1], load_sem.at[1]),
+        pltpu.make_async_copy(tab_hbm, tab, load_sem.at[0]),
+        pltpu.make_async_copy(k_hbm, raw.at[0], load_sem.at[1]),
+        pltpu.make_async_copy(v_hbm, raw.at[1], load_sem.at[2]),
         pltpu.make_async_copy(q_hbm, q_raw, load_sem.at[2]),
-        pltpu.make_async_copy(lengths_hbm, lengths, load_sem.at[4]),
+        pltpu.make_async_copy(lengths_hbm, lengths, load_sem.at[3]),
     ]
     for load in loads[:3]:
         load.start()
@@ -134,11 +135,12 @@
         return remote(some(1, 1, last, 1), some(1, 3, last, 1), z_send.at[1], x_recv.at[0], "seq", above)
 
     def lend_across():
-        return remote(some(1, 3, last, 1), some(1, 4, last, 1), d_send.at[1], x_recv.at[1], "seq", other)
+        return remote(some(1, 3, last, 1), some(1, 4, last, 1), d_send.at[1], x_recv.at[0], "seq", other)
 
     def cross_up(j):
         h = last - 1 + j
-        return remote(some(1, 3, h, 1), some(1, 4, h, 1), z_send.at[1], x_recv.at[2 + j], "seq", me + 1)
+        landed = x_recv.at[1] if j else z_recv.at[up_cuts[-1][-1][0]]
+        return remote(some(1, 3, h, 1), some(1, 4, h, 1), z_send.at[1], landed, "seq", me + 1)
 
     half = heads // 2
 
@@ -169,8 +171,11 @@
         for cut in cuts[: len(cuts) - short]:
             up(kind, hop, cut).start()
 
-    loads[0].wait()
-    loads[1].wait()
+    def loaded(sem, *sizes):
+        view = stage.at[0 : sum(sizes) // (4 * width)]
+        pltpu.make_async_copy(view, view, sem).wait()
+
+    loaded(load_sem.at[0], 2 * rows * wide * width, 4 * 2 * tab.shape[1] * width)
     cos_b = tab[0, pl.ds(rows + me, 1), :]
     sin_b = tab[1, pl.ds(rows + me, 1), :]
     turn[0] = tab[0, 0:rows, :] * cos_b - tab[1, 0:rows, :] * sin_b
@@ -220,7 +225,7 @@
         key_at = lax.broadcasted_iota(jnp.int32, (rows, rows), 1) - d * rows
         bias[d] = jnp.where((key_at >= low) & (key_at <= query_at), 0.0, masked)
 
-    loads[4].wait()
+    loaded(load_sem.at[2], 2 * rows * heads * width, 2 * rows * q_heads * width)
     stage[...] = q_raw[...].astype(jnp.float32).reshape(rows * q_heads, width)
     scale = score_scale * math.log2(math.e)
 
@@ -232,7 +237,6 @@
 
     each(0, heads, turn_q)
 
-    loads[3].wait()
     stage[0 : rows * heads, :] = raw[1].astype(jnp.float32).reshape(rows * heads, width)
 
     def move_v(h):
@@ -356,7 +360,7 @@
         return remote(mine2, parts_dp.at[dp], p_sem.at[0], p_sem.at[1], "dp", lax.rem(dp + j, n_dp))
 
     def tell(j):
-        return remote(told, news, t_sem.at[0], t_sem.at[1], "seq", j)
+        return remote(told, news, s_sem.at[0], s_sem.at[1], "seq", j)
 
     @pl.when(me > 0)
     def _():
@@ -429,6 +433,7 @@
                 if j == 0:
                     lend_up().wait_recv()
                     lend_across().start()
+                    tops[last] = tops[last] + blend(last, (reach - 1,))
 
             cross_up(0).wait_recv()
             take_cut(1, 1, acrosses[3])
@@ -439,6 +444,7 @@
 
         @pl.when(second)
         def _():
+            tops[last] = tops[last] + blend(last, (reach - 1,))
             for j in range(4):
                 up(1, 1, ups[j]).wait_recv()
                 across(1, 1, 2, acrosses[j]).start()
@@ -469,7 +475,7 @@
         news[...] = whole
         each(1, n, lambda j: tell(j).start())
         remote(peers, peers, p_sem.at[0], p_sem.at[1], "seq", other).wait_send()
-        remote(others, others, t_sem.at[0], t_sem.at[1], "seq", other).wait_send()
+        remote(others, others, s_sem.at[0], s_sem.at[1], "seq", other).wait_send()
 
     @pl.when(me > 0)
     def _():
@@ -496,14 +502,12 @@
         @pl.when(first)
         def _():
             cross_up(1).wait_recv()
-            mix(last)
 
         @pl.when(second)
         def _():
             lend_across().wait_recv()
-            mix(last)
-
-    out[...] = spread[...].reshape(rows, q_heads, width).astype(jnp.bfloat16)
+
+        give(last, tops[last] + blend(last, (reach,)))
 
     pl.when(first & has_above & (chip >= 1))(lambda: sent(kv.at[1, 0, 0:last], z_send.at[1]))
     pl.when(second & has_above & (chip >= 1))(lambda: sent(kv.at[1, 0:3, 0 : (heads + 1) // 3], z_send.at[1]))
@@ -511,16 +515,21 @@
     pl.when(second & (chip >= 2))(lambda: sent(kv.at[1, 0, 0:last], d_send.at[1]))
 
 
-def place(held, z_held, out, z_out, z_one, sem):
-    copies = [
-        pltpu.make_async_copy(held, out, sem.at[0]),
-        pltpu.make_async_copy(z_one, z_out, sem.at[1]),
-    ]
-    copies[0].start()
+def place(held, z_held, out, z_out, rounded, z_one, sem):
+    rows, q_heads, width = out.shape
+    part = rows // PARTS
+    for i in range(PARTS):
+        at = slice(i * part, (i + 1) * part)
+        x = held[i * part * q_heads : (i + 1) * part * q_heads, :]
+        rounded[at] = x.reshape(part, q_heads, width).astype(jnp.bfloat16)
+        pltpu.make_async_copy(rounded.at[at], out.at[at], sem.at[i]).start()
     z_one[...] = z_held[0:1, 0:1]
-    copies[1].start()
-    for copy in copies:
-        copy.wait()
+    z_copy = pltpu.make_async_copy(z_one, z_out, sem.at[PARTS])
+    z_copy.start()
+    for i in range(PARTS):
+        at = slice(i * part, (i + 1) * part)
+        pltpu.make_async_copy(rounded.at[at], out.at[at], sem.at[i]).wait()
+    z_copy.wait()
 
 
 def shards(queries, keys, values, lengths):
@@ -539,7 +548,7 @@
     out, z = pl.pallas_call(
         functools.partial(body, n, n_dp, reach),
         out_shape=(
-            pltpu.VMEM((rows, q_heads, width), jnp.bfloat16),
+            pltpu.VMEM((rows * q_heads, width), jnp.float32),
             pltpu.VMEM((8, width), jnp.float32),
         ),
         in_specs=[anywhere] * 5,
@@ -551,7 +560,6 @@
             pltpu.VMEM((rows, q_heads, width), jnp.bfloat16),
             pltpu.VMEM((rows, heads, width), jnp.bfloat16),
             pltpu.VMEM((2, rows, heads, width), jnp.bfloat16),
-            pltpu.VMEM((rows * q_heads, width), jnp.float32),
             pltpu.VMEM((rows * q_heads, width), jnp.float32),
             pltpu.VMEM((heads, group * rows, width), jnp.bfloat16),
             pltpu.VMEM((2, reach + 1, heads, rows, width), jnp.bfloat16),
@@ -566,12 +574,11 @@
             pltpu.VMEM((n_dp, 8, width), jnp.float32),
             pltpu.VMEM((8, width), jnp.float32),
             pltpu.VMEM((8, width), jnp.float32),
-            dma((6,)),
+            dma((4,)),
             dma((2,)),
             dma((sum(len(cuts) for row in UP for cuts in row),)),
             dma((2,)),
             dma((sum(len(cuts) for row in ACROSS for cuts in row),)),
-            dma((4,)),
             dma((2,)),
             dma((2,)),
             dma((2,)),
@@ -589,7 +596,9 @@
         ),
         in_specs=[vmem, vmem],
         out_specs=(anywhere, anywhere),
-        scratch_shapes=[pltpu.VMEM((1, 1), jnp.float32), dma((2,))],
+        scratch_shapes=[
+            pltpu.VMEM((rows, q_heads, width), jnp.bfloat16), pltpu.VMEM((1, 1), jnp.float32), dma((PARTS + 1,))
+        ],
         compiler_params=pltpu.CompilerParams(vmem_limit_bytes=4 * 1024 * 1024),
         name="place",
     )(out, z)

time: 50.3 us -> 50.1 us (level)
  no operation moved by 1% of the time
where the time goes in v4:
time: 50.1 us; the launch traced here: 49.9 us
  Pallas kernels  49.3 us (98%)
  between operations  0.64 us (1%)
    pallas_call x1, Pallas kernels, shards(): pl.pallas_call(functools.partial(body, n, n_dp, reach), out_shape=(pltpu....  48.3 us
    pallas_call x1, Pallas kernels, shards(): pl.pallas_call(place, out_shape=(jax.ShapeDtypeStruct((rows, q_heads, wid...  1.03 us

profile of v4, /device:TPU:16, one launch (start us, length us, event | category | flops | bytes accessed | tf_op | source)
XLA Modules:
  0.0 49.9 jit_solution(5845225929490900242)
XLA Ops:
  0.6 48.3 %attend.1 = (f32[4096,128]{1,0:T(8,128)S(1)}, f32[8,128]{1,0:T(8,128)S(1)}) custom-call(s32[1,8]{1,0:T(1,128)} %lengths_hbm.1, bf16[256,16,128]{2,1,0:T(8,128)(2,1)} %bitcast.5, bf16[256,8,128]{2,1,0:T(8,128)(2,1)} %bitcast.6, bf16[256,8,128]{2,1,0:T(8,128)(2,1)} %bitcast.7, f32[2,264,128]{2,1,0:T(8,128)} %constant.2.clone.tab_hbm), custom_call_target="tpu_custom_call" | custom-call | tf_op jit(solution)/shard_map/attend/pallas_call | solution.py:548
  48.9 1.0 %place.1 = (bf16[256,16,128]{2,1,0:T(8,128)(2,1)}, f32[1,1]{1,0:T(1,128)}) custom-call(f32[4096,128]{1,0:T(8,128)S(1)} %get-tuple-element.6.held, f32[8,128]{1,0:T(8,128)S(1)} %get-tuple-element.7.z_held), custom_call_target="tpu_custom_call" | custom-call | tf_op jit(solution)/shard_map/place/pallas_call | solution.py:591
